TPU v7x, 256 devices: a whole 4x4x8 slice. The times are simulated.
256 devices in a mesh: row: 16 (over z_hi, y, core), col: 16 (over x, z_lo).
Axes of the slice: x: 4, y: 4, z: 8 (z_hi: 2, z_lo: 4; z = z_hi * 4 + z_lo), core: 2. Of those that a mesh axis runs over, the one named last changes fastest.
Arguments:
- series: float32 [16384, 2048], P(('row', 'col'))
- lengths: int32 [16384], P(('row', 'col')), may hold values from 512 to 2048
- starts: int32 [16384], P(('row', 'col')), may hold values from 0 to 1536, as said below
Outputs:
- correlation: float32 [16384, 16384], P('row', 'col')
Inputs may be any that keep to these rules, and one draw needn't show every extreme that they name: starts[s] + lengths[s] <= 2048 for every series.
All inputs are finite; a program needn't handle non-finite values.
Results may differ from a plain program's by a relative error of at most 0.0012.
Values may be sent and summed in bfloat16 or wider, within the bound.
A program may use at most 64 MiB of HBM per device.

v0:
```python
import functools
import math

import jax
import jax.numpy as jnp
from jax import lax
from jax.experimental import pallas as pl
from jax.experimental.pallas import tpu as pltpu
from jax.sharding import PartitionSpec as P

LANES = 128
PANEL_LAG = 1.2
PIECES = 4
BLOCKS = 1
LIMIT = 32
MESH = pl.DeviceIdType.MESH


def column_of(row_values):
    n = row_values.shape[1]
    here = lax.broadcasted_iota(jnp.int32, (n, n), 0)
    there = lax.broadcasted_iota(jnp.int32, (n, n), 1)
    picked = jnp.where(here == there, jnp.broadcast_to(row_values, (n, n)), 0)
    return jnp.sum(picked, axis=1, keepdims=True)


def normalize(series, lengths, starts):
    positions = lax.broadcasted_iota(jnp.int32, series.shape, 1)
    inside = (positions >= starts) & (positions < starts + lengths)
    valid_count = lengths.astype(jnp.float32)
    average = jnp.sum(jnp.where(inside, series, 0.0), axis=1, keepdims=True) / valid_count
    centered = jnp.where(inside, series - average, 0.0)
    variance = jnp.sum(centered * centered, axis=1, keepdims=True) / valid_count
    return (centered / jnp.sqrt(valid_count * (variance + 1e-06))).astype(jnp.bfloat16)


def pieces_of(steps, slow, fast, count):
    tiles = steps // LANES
    share = 0.0
    if slow > 1 and fast > 1:
        share = ((fast - 1) * slow - (slow - 1)) / (2 * (slow - 1) * (fast - 1))
    fast_tiles = max(0, min(tiles - 1, round(share * tiles)))
    edges = []
    if fast_tiles:
        parts = max(1, round(count * fast_tiles / tiles))
        cuts = [fast_tiles * i // parts for i in range(parts + 1)]
        edges += [(lo, hi, True) for lo, hi in zip(cuts, cuts[1:])]
    rest = tiles - fast_tiles
    parts = max(1, min(rest, count - len(edges)))
    cuts = [fast_tiles + rest * i // parts for i in range(parts + 1)]
    edges += [(lo, hi, False) for lo, hi in zip(cuts, cuts[1:])]
    return [(lo * LANES, hi * LANES, first) for lo, hi, first in edges]


def kernel(
    row_total, slow, fast, pieces,
    series_ref, windows_ref, slab,
    recv, send, tree_recv, tree_send,
):
    rows_dev = series_ref.shape[0]
    col_total = slow * fast
    bits = row_total.bit_length() - 1
    r = lax.axis_index("row")
    c = lax.axis_index("col")
    a, b = c // fast, c % fast
    root = c * row_total // col_total
    first = c * row_total % col_total

    def flip(k):
        return r + 2**k * (1 - 2 * (r // 2**k % 2))

    low, same = [1], []
    for k in range(bits):
        bit, root_bit = r // 2**k % 2, root // 2**k % 2
        same.append(1 - (bit + root_bit - 2 * bit * root_bit))
        low.append(low[-1] * same[-1])
    is_root = low[bits] == 1

    def as_int(x):
        return jnp.where(x, 1, 0)

    steps_to = {
        "slow+": (a < slow - 1, c + fast),
        "slow-": (a > 0, c - fast),
        "fast+": (b < fast - 1, c + 1),
        "fast-": (b > 0, c - 1),
    }

    barrier = pltpu.get_barrier_semaphore()
    expected = 0
    for there, target in steps_to.values():
        expected = expected + as_int(there)

        @pl.when(there)
        def _(target=target):
            pl.semaphore_signal(
                barrier, inc=1, device_id={"row": r, "col": target}, device_id_type=MESH
            )

    for k in range(bits):
        expected = expected + low[k]

        @pl.when(jnp.asarray(low[k]) == 1)
        def _(k=k):
            pl.semaphore_signal(
                barrier, inc=1, device_id={"row": flip(k), "col": c}, device_id_type=MESH
            )

    slab[c] = normalize(
        series_ref[...], column_of(windows_ref[0:1]), column_of(windows_ref[1:2])
    )
    pl.semaphore_wait(barrier, expected)

    started = []

    def go(condition, copy_of):
        @pl.when(condition)
        def _():
            copy_of().start()

        started.append((condition, copy_of))

    def part(slot, piece):
        lo, hi, _ = pieces[piece]
        return slab.at[slot, :, pl.ds(lo, hi - lo)]

    def gather_copy(slot, piece, way):
        return pltpu.make_async_remote_copy(
            src_ref=part(slot, piece),
            dst_ref=part(slot, piece),
            send_sem=send.at[list(steps_to).index(way), slot, piece],
            recv_sem=recv.at[slot, piece],
            device_id={"row": r, "col": steps_to[way][1]},
            device_id_type=MESH,
        )

    def tree_copy(source, j, piece, k):
        return pltpu.make_async_remote_copy(
            src_ref=part(source, piece),
            dst_ref=part(col_total + j, piece),
            send_sem=tree_send.at[k, j, piece],
            recv_sem=tree_recv.at[j, piece],
            device_id={"row": flip(k), "col": c},
            device_id_type=MESH,
        )

    def ways(da, db, fast_first):
        main, cross = (db, da) if fast_first else (da, db)
        names = ("fast", "slow") if fast_first else ("slow", "fast")
        out = []
        if cross == 0:
            if main <= 0:
                out.append(names[0] + "+")
            if main >= 0:
                out.append(names[0] + "-")
            out += [names[1] + "+", names[1] + "-"]
        else:
            out.append(names[1] + ("+" if cross < 0 else "-"))
        return out

    def arrive(da, db, piece):
        slot = c + da * fast + db
        valid = (a + da >= 0) & (a + da < slow) & (b + db >= 0) & (b + db < fast)
        if (da, db) != (0, 0):

            @pl.when(valid)
            def _():
                gather_copy(slot, piece, "slow+").wait_recv()

        for way in ways(da, db, pieces[piece][2]):
            go(valid & steps_to[way][0], functools.partial(gather_copy, slot, piece, way))
        j = slot - first
        for k in range(bits):
            go(
                valid & is_root & (j >= 0) & (j < row_total),
                functools.partial(tree_copy, slot, j, piece, k),
            )

    def arrive_panel(da, db, piece):
        j = c + da * fast + db - first
        valid = (a + da >= 0) & (a + da < slow) & (b + db >= 0) & (b + db < fast)
        valid = valid & jnp.logical_not(is_root) & (j >= 0) & (j < row_total)

        @pl.when(valid)
        def _():
            tree_copy(col_total + j, j, piece, 0).wait_recv()

        for k in range(bits - 1):
            go(
                valid & (jnp.asarray(low[k + 1]) == 1),
                functools.partial(tree_copy, col_total + j, j, piece, k),
            )

    events = []
    for piece in range(len(pieces)):
        for da in range(1 - slow, slow):
            for db in range(1 - fast, fast):
                distance = abs(da) + abs(db)
                events.append((distance, piece, arrive, da, db))
                events.append((distance + PANEL_LAG, piece, arrive_panel, da, db))
    events.sort(key=lambda event: event[:2])
    for _, piece, action, da, db in events:
        action(da, db, piece)

    for condition, copy_of in started:

        @pl.when(condition)
        def _(copy_of=copy_of):
            copy_of().wait_send()


def multiply(row_total, slab, out_ref):
    total, rows_dev, steps = slab.shape
    col_total = total - row_total
    c = lax.axis_index("col")
    root = c * row_total // col_total
    base = jnp.where(
        lax.axis_index("row") == root, c * row_total % col_total, col_total
    )
    block = out_ref.shape[0] // rows_dev
    left = slab[pl.ds(pl.program_id(0) * block, block)].reshape(block * rows_dev, steps)
    group = max(1, min(row_total, 256 // rows_dev))
    for g in range(row_total // group):
        right = slab[pl.ds(base + g * group, group)].reshape(group * rows_dev, steps)
        out_ref[:, g * group * rows_dev : (g + 1) * group * rows_dev] = lax.dot_general(
            left, right, (((1,), (1,)), ((), ())), preferred_element_type=jnp.float32
        )


def on_device(row_total, col_total, series, lengths, starts):
    rows_dev, steps = series.shape
    fast = 2 ** (int(math.log2(col_total)) // 2)
    slow = col_total // fast
    pieces = pieces_of(steps, slow, fast, PIECES)
    bits = row_total.bit_length() - 1
    vmem = pl.BlockSpec(memory_space=pltpu.VMEM)
    slab = pl.pallas_call(
        functools.partial(kernel, row_total, slow, fast, pieces),
        out_shape=jax.ShapeDtypeStruct(
            (col_total + row_total, rows_dev, steps), jnp.bfloat16
        ),
        in_specs=[vmem] * 2,
        out_specs=vmem,
        scratch_shapes=[
            pltpu.SemaphoreType.DMA((col_total, len(pieces))),
            pltpu.SemaphoreType.DMA((4, col_total, len(pieces))),
            pltpu.SemaphoreType.DMA((row_total, len(pieces))),
            pltpu.SemaphoreType.DMA((bits, row_total, len(pieces))),
        ],
        compiler_params=pltpu.CompilerParams(
            collective_id=0, has_side_effects=True, vmem_limit_bytes=LIMIT * 2**20
        ),
    )(series, jnp.stack([lengths, starts]))
    rows, columns = col_total * rows_dev, row_total * rows_dev
    blocks = BLOCKS
    return pl.pallas_call(
        functools.partial(multiply, row_total),
        grid=(blocks,),
        out_shape=jax.ShapeDtypeStruct((rows, columns), jnp.float32),
        in_specs=[vmem],
        out_specs=pl.BlockSpec((rows // blocks, columns), lambda i: (i, 0)),
        compiler_params=pltpu.CompilerParams(vmem_limit_bytes=LIMIT * 2**20),
    )(slab)


def solution(mesh):
    in_specs = (P(("row", "col"), None), P(("row", "col")), P(("row", "col")))
    out_specs = P("row", "col")
    return jax.shard_map(
        functools.partial(on_device, mesh.shape["row"], mesh.shape["col"]),
        mesh=mesh, in_specs=in_specs, out_specs=out_specs, check_vma=False,
    )
```

profile of v0, /device:TPU:71, one launch (start us, length us, event | category | flops | bytes accessed | tf_op | source)
XLA Modules:
  0.0 140.7 jit_solution(13699939066035689524)
XLA Ops:
  0.0 0.7 pad_add_fusion.windows_ref
  0.7 0.0 copy-start
  0.7 1.0 copy-done
  1.7 132.4 %shard_map.37.slab = bf16[32,64,2048]{2,1,0:T(8,128)(2,1)S(1)} custom-call(f32[64,2048]{1,0:T(8,128)S(1)} %copy-done, s32[2,64]{1,0:T(2,128)S(1)} %pad_add_fusion.windows_ref), custom_call_target="tpu_custom_call" | custom-call | tf_op jit(solution)/shard_map/pallas_call | solution.py:237
  134.1 6.6 %shard_map.38 = f32[1024,1024]{1,0:T(8,128)} custom-call(bf16[32,64,2048]{2,1,0:T(8,128)(2,1)S(1)} %shard_map.37.slab), custom_call_target="tpu_custom_call" | custom-call | tf_op jit(solution)/shard_map/pallas_call | solution.py:256
Async XLA Ops:
  0.7 1.0 copy-start
where the time goes:
time: 141 us
  Pallas kernels  139 us (99%)
    pallas_call x1, Pallas kernels, on_device(): pl.pallas_call(functools.partial(kernel, row_total, slow, fast, pieces),...  132 us
    pallas_call x1, Pallas kernels, on_device(): pl.pallas_call(functools.partial(multiply, row_total), grid=(blocks,), ou...  6.55 us

commit v1 on v0

v1 whole, which is shorter than its diff:
```python
import functools

import jax
import jax.numpy as jnp
from jax import lax
from jax.experimental import pallas as pl
from jax.experimental.pallas import tpu as pltpu
from jax.sharding import PartitionSpec as P

LANES = 128
SIDE = 4
ALONG_Z = 7
LIMIT = 32
MESH = pl.DeviceIdType.MESH
ORDER = (
    0, 1, 11, 54, 112, 155, 12, 113, 55, 156, 13, 114, 137, 29, 181, 66, 56, 157, 138, 30,
    14, 40, 127, 81, 167, 57, 15, 182, 148, 47, 16, 196, 8, 53, 206, 204, 9, 31, 67, 115,
    158, 41, 116, 208, 10, 109, 154, 209, 32, 110, 95, 117, 17, 27, 224, 58, 18, 5, 68,
    139, 52, 183, 225, 207, 82, 205, 140, 28, 6, 111, 39, 168, 19, 212, 197, 118, 216, 159,
    96, 7, 48, 135, 64, 119, 69, 106, 153, 136, 107, 179, 184, 210, 128, 228, 83, 79, 232,
    213, 120, 217, 65, 165, 70, 180, 169, 2, 185, 80, 20, 84, 21, 51, 22, 194, 108, 3, 166,
    59, 33, 34, 170, 4, 195, 198, 199, 211, 93, 94, 149, 25, 26, 46, 97, 98, 233, 220, 229,
    226, 42, 38, 121, 122, 123, 126, 160, 218, 103, 104, 105, 152, 214, 71, 72, 62, 63,
    141, 142, 177, 178, 186, 187, 227, 147, 85, 77, 78, 133, 134, 86, 221, 236, 163, 164,
    171, 172, 125, 129, 43, 219, 23, 24, 37, 200, 201, 192, 193, 91, 92, 99, 100, 234, 35,
    36, 49, 215, 230, 45, 237, 60, 61, 175, 176, 222, 143, 144, 75, 76, 131, 146, 235, 130,
    124, 73, 74, 132, 231, 188, 189, 161, 162, 150, 190, 191, 87, 88, 89, 90, 223, 173,
    174, 202, 203, 44, 50, 238, 101, 102, 145, 239, 151,
)


def column_of(row_values):
    n = row_values.shape[1]
    here = lax.broadcasted_iota(jnp.int32, (n, n), 0)
    there = lax.broadcasted_iota(jnp.int32, (n, n), 1)
    picked = jnp.where(here == there, jnp.broadcast_to(row_values, (n, n)), 0)
    return jnp.sum(picked, axis=1, keepdims=True)


def normalize(series, lengths, starts):
    positions = lax.broadcasted_iota(jnp.int32, series.shape, 1)
    inside = (positions >= starts) & (positions < starts + lengths)
    valid_count = lengths.astype(jnp.float32)
    average = jnp.sum(jnp.where(inside, series, 0.0), axis=1, keepdims=True) / valid_count
    centered = jnp.where(inside, series - average, 0.0)
    variance = jnp.sum(centered * centered, axis=1, keepdims=True) / valid_count
    return (centered / jnp.sqrt(valid_count * (variance + 1e-06))).astype(jnp.bfloat16)


def pick(condition, a, b):
    if isinstance(condition, (bool, int)):
        return a if condition else b
    return jnp.where(condition, a, b)


def columns_of(steps):
    half, along = steps // 2, ALONG_Z * LANES
    return [
        (0, along), (along, half), (half, half + along), (half + along, steps),
        (0, half), (half, steps),
    ]


def events_of(r, c):
    n = SIDE
    zh, y, k = r // (2 * n), r // 2 % n, r % 2
    x, z = c // n, c % n

    def row_at(zh, y, k):
        return zh * (2 * n) + y % n * 2 + k

    def col_at(x, z):
        return x % n * n + z

    def c_y(row):
        return row // 2 % n

    events = []
    go = {
        "x+": (True, r, col_at(x + 1, z)),
        "x-": (True, r, col_at(x + n - 1, z)),
        "z+": (z < n - 1, r, c + 1),
        "z-": (z > 0, r, c - 1),
    }

    home_x, home_z = r // n, r % n
    d = (home_x - x + n) % n
    core = d % 2
    target = pick(d == 0, n * n + c, 2 * n * n + d // 3)
    here = (z == home_z) & (z == 0) & (core == k)
    for half in (4, 5):
        sends = [
            (True, c, target, half, row_at((zh + 1) % 2, y + z, core), col_at(x, home_z)),
            (1 - pick(here, 1, 0) == 1, c, target, half, row_at(zh, y + z, core),
             col_at(x, home_z)),
            (here, c, target, half, None, None),
            (here & (d != 0), c, n * n + c, half, r, col_at(home_x, z)),
        ]
        for row in (row_at(zh, y + 1, k), row_at(zh, y + n - 1, k), row_at(zh, y, 1 - k)):
            sends.append((here & (d == 0), n * n + c, n * n + c, half, row, c))
        events.append((("own", half), True, None, sends, []))

    for piece in range(4):
        first, second = piece % 2 == 0, piece // 2
        for dx in (0, 3, 1, 2):
            for dz in range(1 - n, n):
                slot = col_at(x + dx, 0) + z + dz
                valid = (z + dz >= 0) & (z + dz < n)
                def ways(*names):
                    return [
                        (go[way][0], slot, slot, piece, go[way][1], go[way][2])
                        for way in names
                    ]

                def add(kind, sends):
                    events.append(
                        ((kind, dx, dz, piece), valid, None, sends, [(slot, piece)])
                    )

                z_ways = (["z+"] if dz <= 0 else []) + (["z-"] if dz >= 0 else [])
                wait = None if dx == 0 and dz == 0 else (slot, piece)
                urgent = ways(*z_ways) if dx == 0 else []
                events.append((("left", dx, dz, piece), valid, wait, urgent, []))
                if first or dz == 0:
                    if dx == 0:
                        add("near", ways("x+" if second == 0 else "x-"))
                        add("side", ways("x-" if second == 0 else "x+"))
                    elif dx == 3 and second == 0:
                        add("far", ways("x+"))
                    elif dx == 1 and second == 1:
                        add("far", ways("x-"))
                if not first and dx != 0:
                    add("over", ways(*z_ways))

    for j in range(2):
        for half in (4, 5):
            d = 2 - k + 2 * j
            slot = 2 * n * n + j
            from_z = (y - c_y((x + d) % n * n + z) + n) % n
            sends = [(True, slot, n * n + x * n + from_z, half, r, col_at(x + d, z))]
            panel = (x + d) % n * n + z
            arrives = (r != panel) | (z != 0)
            valid = arrives if j == 0 else arrives & (k == 1)
            events.append((("pass", j, half), valid, (slot, half), sends, []))

    for j in range(2):
        for dy in (0, 3, 1, 2):
            for half in (4, 5):
                from_z = (y + dy - c_y(c) + n) % n
                slot = n * n + (x + k + 2 * j) % n * n + from_z
                up = (True, slot, slot, half, row_at(zh, y + 1, k), c)
                down = (True, slot, slot, half, row_at(zh, y + n - 1, k), c)
                across = (True, slot, slot, half, row_at(zh, y, 1 - k), c)
                sends = []
                if dy == 0:
                    sends = [up, down] if half == 4 else [down, up]
                elif dy == 3 and half == 4:
                    sends = [up]
                elif dy == 1 and half == 5:
                    sends = [down]
                valid = True
                if dy == 0 and j == 0:
                    valid = (k == 1) | (r != c) | (z != 0)
                events.append(
                    (("right", j, dy, half), valid, (slot, half), sends + [across], [])
                )
                slot = n * n + (x + 1 - k + 2 * j) % n * n + from_z
                events.append((("across", j, dy, half), True, (slot, half), [], []))
    if ORDER:
        events = [events[i] for i in ORDER]
    return events


def peers_of(r, c):
    n = SIDE
    zh, y, k = r // (2 * n), r // 2 % n, r % 2
    x, z = c // n, c % n
    around = [(True, r, (c + n) % (n * n)), (True, r, (c + 3 * n) % (n * n))]
    around += [(z < n - 1, r, c + 1), (z > 0, r, c - 1)]
    for dy in (1, n - 1):
        around.append((True, zh * 2 * n + (y + dy) % n * 2 + k, c))
    around.append((True, r + 1 - 2 * k, c))
    around.append((k == 0, r, (c + 2 * n) % (n * n)))
    home_x, home_z = r // n, r % n
    core = (home_x - x + n) % n % 2
    into, out = list(around), list(around)
    for group in range(2):
        row, col = group * 2 * n + (y + z) % n * 2 + core, x * n + home_z
        out.append(((row != r) | (col != c), row, col))
        row = (x + k + 2 * group) % n * n + z
        col = x * n + (y - row // 2 % n + n) % n
        into.append(((row != r) | (col != c), row, col))
    return into, out


def kernel(columns, series_ref, windows_ref, slab, recv, send):
    r = lax.axis_index("row")
    c = lax.axis_index("col")
    n = SIDE

    into, out = peers_of(r, c)
    barrier = pltpu.get_barrier_semaphore()
    for condition, row, col in into:

        @pl.when(condition)
        def _(row=row, col=col):
            pl.semaphore_signal(
                barrier, inc=1, device_id={"row": row, "col": col}, device_id_type=MESH
            )

    slab[c] = normalize(
        series_ref[...], column_of(windows_ref[0:1]), column_of(windows_ref[1:2])
    )
    expected = sum(jnp.where(condition, 1, 0) for condition, _, _ in out)
    pl.semaphore_wait(barrier, expected)

    started = []

    def part(slot, piece):
        lo, hi = columns[piece]
        return slab.at[slot, :, pl.ds(lo, hi - lo)]

    def copy_of(index, source, target, piece, row, col):
        return pltpu.make_async_remote_copy(
            src_ref=part(source, piece),
            dst_ref=part(target, piece),
            send_sem=send.at[index],
            recv_sem=recv.at[target, piece],
            device_id={"row": row, "col": col},
            device_id_type=MESH,
        )

    def guarded(condition, do):
        if condition is True:
            do()
        else:
            pl.when(condition)(do)

    def handle(wait, sends):
        if wait is not None:

            def receive():
                copy_of(0, wait[0], wait[0], wait[1], r, c).wait_recv()

            receive()
        for condition, source, target, piece, row, col in sends:
            if row is None:

                def keep(source=source, target=target, piece=piece):
                    part(target, piece)[...] = part(source, piece)[...]

                guarded(condition, keep)
                continue
            index = len(started)
            copy = functools.partial(copy_of, index, source, target, piece, row, col)
            guarded(condition, lambda copy=copy: copy().start())
            started.append((condition, copy))

    for name, condition, wait, sends, _ in events_of(r, c):
        before = len(started)
        guarded(condition, lambda: handle(wait, sends))
        if condition is not True:
            started[before:] = [
                (condition if own is True else condition & own, copy)
                for own, copy in started[before:]
            ]

    for condition, copy in started:
        guarded(condition, lambda copy=copy: copy().wait_send())


def count_sends():
    return sum(len(event[3]) for event in events_of(0, 0))


def multiply(slab, out_ref):
    half, rows_dev, steps = SIDE * SIDE, slab.shape[1], slab.shape[2]
    left = slab[:half].reshape(half * rows_dev, steps)
    group = max(1, 256 // rows_dev)
    for g in range(half // group):
        right = slab[half + g * group : half + (g + 1) * group]
        out_ref[:, g * group * rows_dev : (g + 1) * group * rows_dev] = lax.dot_general(
            left, right.reshape(group * rows_dev, steps), (((1,), (1,)), ((), ())),
            preferred_element_type=jnp.float32,
        )


def on_device(series, lengths, starts):
    rows_dev, steps = series.shape
    blocks = SIDE * SIDE
    vmem = pl.BlockSpec(memory_space=pltpu.VMEM)
    columns = columns_of(steps)
    slots = 2 * blocks + 2
    slab = pl.pallas_call(
        functools.partial(kernel, columns),
        out_shape=jax.ShapeDtypeStruct((slots, rows_dev, steps), jnp.bfloat16),
        in_specs=[vmem] * 2,
        out_specs=vmem,
        scratch_shapes=[
            pltpu.SemaphoreType.DMA((slots, len(columns))),
            pltpu.SemaphoreType.DMA((count_sends(),)),
        ],
        compiler_params=pltpu.CompilerParams(
            collective_id=0, has_side_effects=True, vmem_limit_bytes=LIMIT * 2**20
        ),
    )(series, jnp.stack([lengths, starts]))
    rows = blocks * rows_dev
    return pl.pallas_call(
        multiply,
        grid=(1,),
        out_shape=jax.ShapeDtypeStruct((rows, rows), jnp.float32),
        in_specs=[vmem],
        out_specs=pl.BlockSpec((rows, rows), lambda i: (i, 0)),
        compiler_params=pltpu.CompilerParams(vmem_limit_bytes=LIMIT * 2**20),
    )(slab)


def solution(mesh):
    in_specs = (P(("row", "col"), None), P(("row", "col")), P(("row", "col")))
    out_specs = P("row", "col")
    return jax.shard_map(
        on_device, mesh=mesh, in_specs=in_specs, out_specs=out_specs, check_vma=False,
    )
```

time: 141 us -> 76 us (0.54)
  the two profiles are of different devices: /device:TPU:71 before, /device:TPU:1 now
where the time goes in v1:
time: 76 us; the launch traced here: 75.5 us
  Pallas kernels  73.8 us (97%)
  local copies, waits for them, and re-layouts  1.04 us (1%)
    pallas_call x1, Pallas kernels, on_device(): pl.pallas_call(functools.partial(kernel, columns), out_shape=jax.ShapeDty...  67.2 us
    pallas_call x1, Pallas kernels, on_device(): pl.pallas_call(multiply, grid=(1,), out_shape=jax.ShapeDtypeStruct((rows,...  6.53 us

profile of v1, /device:TPU:1, one launch (start us, length us, event | category | flops | bytes accessed | tf_op | source)
XLA Modules:
  0.0 75.5 jit_solution(15653690371411779881)
XLA Ops:
  0.0 0.7 pad_add_fusion.windows_ref
  0.7 0.0 copy-start
  0.7 1.0 %copy-done = f32[64,2048]{1,0:T(8,128)S(1)} copy-done((f32[64,2048]{1,0:T(8,128)S(1)}, f32[64,2048]{1,0:T(8,128)}, u32[]{:S(2)}) %copy-start) | copy-done | bytes 524312
  1.7 67.2 %shard_map.37.slab = bf16[34,64,2048]{2,1,0:T(8,128)(2,1)S(1)} custom-call(f32[64,2048]{1,0:T(8,128)S(1)} %copy-done, s32[2,64]{1,0:T(2,128)S(1)} %pad_add_fusion.windows_ref), custom_call_target="tpu_custom_call" | custom-call | tf_op jit(solution)/shard_map/pallas_call | solution.py:294
  69.0 6.5 %shard_map.38 = f32[1024,1024]{1,0:T(8,128)} custom-call(bf16[34,64,2048]{2,1,0:T(8,128)(2,1)S(1)} %shard_map.37.slab), custom_call_target="tpu_custom_call" | custom-call | tf_op jit(solution)/shard_map/pallas_call | solution.py:308
Async XLA Ops:
  0.7 1.0 %copy-start = (f32[64,2048]{1,0:T(8,128)S(1)}, f32[64,2048]{1,0:T(8,128)}, u32[]{:S(2)}) copy-start(f32[64,2048]{1,0:T(8,128)} %series_ref.1) | copy-start | bytes 1572868

commit v2 on v1

--- a/solution.py
+++ b/solution.py
@@ -11,21 +11,22 @@
 SIDE = 4
 ALONG_Z = 7
 LIMIT = 32
+OUT_PARTS = 4
 MESH = pl.DeviceIdType.MESH
 ORDER = (
-    0, 1, 11, 54, 112, 155, 12, 113, 55, 156, 13, 114, 137, 29, 181, 66, 56, 157, 138, 30,
-    14, 40, 127, 81, 167, 57, 15, 182, 148, 47, 16, 196, 8, 53, 206, 204, 9, 31, 67, 115,
-    158, 41, 116, 208, 10, 109, 154, 209, 32, 110, 95, 117, 17, 27, 224, 58, 18, 5, 68,
-    139, 52, 183, 225, 207, 82, 205, 140, 28, 6, 111, 39, 168, 19, 212, 197, 118, 216, 159,
-    96, 7, 48, 135, 64, 119, 69, 106, 153, 136, 107, 179, 184, 210, 128, 228, 83, 79, 232,
-    213, 120, 217, 65, 165, 70, 180, 169, 2, 185, 80, 20, 84, 21, 51, 22, 194, 108, 3, 166,
-    59, 33, 34, 170, 4, 195, 198, 199, 211, 93, 94, 149, 25, 26, 46, 97, 98, 233, 220, 229,
-    226, 42, 38, 121, 122, 123, 126, 160, 218, 103, 104, 105, 152, 214, 71, 72, 62, 63,
-    141, 142, 177, 178, 186, 187, 227, 147, 85, 77, 78, 133, 134, 86, 221, 236, 163, 164,
-    171, 172, 125, 129, 43, 219, 23, 24, 37, 200, 201, 192, 193, 91, 92, 99, 100, 234, 35,
-    36, 49, 215, 230, 45, 237, 60, 61, 175, 176, 222, 143, 144, 75, 76, 131, 146, 235, 130,
-    124, 73, 74, 132, 231, 188, 189, 161, 162, 150, 190, 191, 87, 88, 89, 90, 223, 173,
-    174, 202, 203, 44, 50, 238, 101, 102, 145, 239, 151,
+    0, 5, 3, 160, 161, 1, 60, 58, 59, 16, 118, 116, 15, 17, 117, 186, 120, 2, 34, 61, 71,
+    72, 19, 201, 119, 86, 113, 172, 20, 208, 18, 14, 12, 68, 114, 99, 200, 115, 144, 36, 4,
+    122, 224, 111, 13, 112, 45, 170, 100, 225, 121, 9, 142, 35, 97, 203, 57, 98, 11, 23,
+    22, 10, 210, 21, 110, 123, 187, 7, 32, 204, 31, 127, 8, 51, 73, 126, 108, 220, 159,
+    226, 109, 84, 56, 26, 153, 6, 216, 80, 184, 174, 83, 140, 199, 25, 62, 63, 147, 202,
+    228, 236, 217, 189, 95, 148, 138, 124, 33, 171, 205, 211, 178, 222, 212, 135, 82, 182,
+    176, 102, 177, 96, 130, 206, 103, 81, 79, 229, 74, 29, 42, 69, 40, 188, 46, 152, 146,
+    167, 94, 232, 28, 213, 197, 41, 139, 30, 175, 38, 137, 101, 87, 143, 162, 214, 237,
+    163, 132, 105, 76, 47, 44, 169, 75, 221, 166, 54, 194, 37, 158, 128, 125, 43, 218, 155,
+    196, 90, 136, 88, 89, 65, 107, 85, 151, 180, 24, 168, 104, 179, 230, 67, 238, 209, 133,
+    92, 191, 234, 185, 70, 91, 183, 198, 227, 223, 157, 215, 66, 231, 55, 207, 77, 106,
+    192, 181, 219, 49, 27, 173, 235, 78, 165, 134, 131, 145, 50, 39, 195, 190, 156, 141,
+    193, 149, 53, 233, 150, 129, 164, 239, 64, 52, 154, 48, 93,
 )
 
 
@@ -83,22 +84,30 @@
         "z-": (z > 0, r, c - 1),
     }
 
-    home_x, home_z = r // n, r % n
-    d = (home_x - x + n) % n
-    core = d % 2
-    target = pick(d == 0, n * n + c, 2 * n * n + d // 3)
-    here = (z == home_z) & (z == 0) & (core == k)
     for half in (4, 5):
-        sends = [
-            (True, c, target, half, row_at((zh + 1) % 2, y + z, core), col_at(x, home_z)),
-            (1 - pick(here, 1, 0) == 1, c, target, half, row_at(zh, y + z, core),
-             col_at(x, home_z)),
-            (here, c, target, half, None, None),
-            (here & (d != 0), c, n * n + c, half, r, col_at(home_x, z)),
-        ]
-        for row in (row_at(zh, y + 1, k), row_at(zh, y + n - 1, k), row_at(zh, y, 1 - k)):
-            sends.append((here & (d == 0), n * n + c, n * n + c, half, row, c))
+        sends = [(z != 0, c, 2 * n * n, half, row_at(zh, y + z, k), c)]
         events.append((("own", half), True, None, sends, []))
+
+    panel = row_at(zh, y + n - z, k)
+    home_x, home_z = panel // n, panel % n
+    core = (home_x + x) % 2
+    here = (home_x == x) & (home_z == z) & (k == 0)
+    for half in (4, 5):
+        for kind in ("moved", "stays"):
+            source = 2 * n * n if kind == "moved" else c
+            slot = n * n + c
+            sends = [
+                (True, source, slot, half, row_at((zh + 1) % 2, y, core),
+                 col_at(home_x, home_z)),
+                (pick(here, 0, 1) == 1, source, slot, half, row_at(zh, y, core),
+                 col_at(home_x, home_z)),
+                (here, source, slot, half, None, None),
+            ]
+            for row in (row_at(zh, y + 2, k), row_at(zh, y + 1, k), row_at(zh, y + n - 1, k),
+                        row_at(zh, y, 1 - k)):
+                sends.append((here, slot, slot, half, row, c))
+            valid, wait = (z != 0, (2 * n * n, half)) if kind == "moved" else (z == 0, None)
+            events.append(((kind, half), valid, wait, sends, []))
 
     for piece in range(4):
         first, second = piece % 2 == 0, piece // 2
@@ -133,17 +142,6 @@
                     add("over", ways(*z_ways))
 
     for j in range(2):
-        for half in (4, 5):
-            d = 2 - k + 2 * j
-            slot = 2 * n * n + j
-            from_z = (y - c_y((x + d) % n * n + z) + n) % n
-            sends = [(True, slot, n * n + x * n + from_z, half, r, col_at(x + d, z))]
-            panel = (x + d) % n * n + z
-            arrives = (r != panel) | (z != 0)
-            valid = arrives if j == 0 else arrives & (k == 1)
-            events.append((("pass", j, half), valid, (slot, half), sends, []))
-
-    for j in range(2):
         for dy in (0, 3, 1, 2):
             for half in (4, 5):
                 from_z = (y + dy - c_y(c) + n) % n
@@ -153,14 +151,11 @@
                 across = (True, slot, slot, half, row_at(zh, y, 1 - k), c)
                 sends = []
                 if dy == 0:
-                    sends = [up, down] if half == 4 else [down, up]
-                elif dy == 3 and half == 4:
-                    sends = [up]
-                elif dy == 1 and half == 5:
-                    sends = [down]
+                    beyond = (True, slot, slot, half, row_at(zh, y + 2, k), c)
+                    sends = [beyond, up, down]
                 valid = True
                 if dy == 0 and j == 0:
-                    valid = (k == 1) | (r != c) | (z != 0)
+                    valid = pick((k == 0) & (panel == c), 0, 1) == 1
                 events.append(
                     (("right", j, dy, half), valid, (slot, half), sends + [across], [])
                 )
@@ -168,6 +163,14 @@
                 events.append((("across", j, dy, half), True, (slot, half), [], []))
     if ORDER:
         events = [events[i] for i in ORDER]
+    waited = set()
+    for i, (name, valid, wait, sends, needs) in enumerate(events):
+        if name[0] in ("left", "near", "side", "far", "over"):
+            own = name[1] == 0 and name[2] == 0
+            first = not own and name[1:] not in waited
+            waited.add(name[1:])
+            arrival = needs[0] if needs else wait
+            events[i] = (name, valid, arrival if first else None, sends, needs)
     return events
 
 
@@ -177,27 +180,43 @@
     x, z = c // n, c % n
     around = [(True, r, (c + n) % (n * n)), (True, r, (c + 3 * n) % (n * n))]
     around += [(z < n - 1, r, c + 1), (z > 0, r, c - 1)]
-    for dy in (1, n - 1):
+    for dy in (1, 2, n - 1):
         around.append((True, zh * 2 * n + (y + dy) % n * 2 + k, c))
     around.append((True, r + 1 - 2 * k, c))
-    around.append((k == 0, r, (c + 2 * n) % (n * n)))
-    home_x, home_z = r // n, r % n
-    core = (home_x - x + n) % n % 2
     into, out = list(around), list(around)
+
+    def row_at(zh, y, k):
+        return zh * (2 * n) + y % n * 2 + k
+
+    out.append((z != 0, row_at(zh, y + z, k), c))
+    into.append((z != 0, row_at(zh, y + n - z, k), c))
+    panel = row_at(zh, y + n - z, k)
     for group in range(2):
-        row, col = group * 2 * n + (y + z) % n * 2 + core, x * n + home_z
+        row, col = row_at(group, y, (panel // n + x) % 2), panel
         out.append(((row != r) | (col != c), row, col))
-        row = (x + k + 2 * group) % n * n + z
-        col = x * n + (y - row // 2 % n + n) % n
+        from_z = (y + n - c // 2 % n) % n
+        row = row_at(c // (2 * n), y, c % 2)
+        col = (x + k + 2 * group) % n * n + from_z
         into.append(((row != r) | (col != c), row, col))
     return into, out
 
 
-def kernel(columns, series_ref, windows_ref, slab, recv, send):
+def kernel(
+    columns, series_hbm, lengths_hbm, starts_hbm, slab,
+    series_ref, lengths_ref, starts_ref, recv, send, load,
+):
     r = lax.axis_index("row")
     c = lax.axis_index("col")
     n = SIDE
 
+    loads = [
+        pltpu.make_async_copy(source, target, load.at[i])
+        for i, (source, target) in enumerate((
+            (lengths_hbm, lengths_ref), (starts_hbm, starts_ref), (series_hbm, series_ref),
+        ))
+    ]
+    for copy in loads:
+        copy.start()
     into, out = peers_of(r, c)
     barrier = pltpu.get_barrier_semaphore()
     for condition, row, col in into:
@@ -208,8 +227,10 @@
                 barrier, inc=1, device_id={"row": row, "col": col}, device_id_type=MESH
             )
 
+    for copy in loads:
+        copy.wait()
     slab[c] = normalize(
-        series_ref[...], column_of(windows_ref[0:1]), column_of(windows_ref[1:2])
+        series_ref[...], column_of(lengths_ref[...]), column_of(starts_ref[...])
     )
     expected = sum(jnp.where(condition, 1, 0) for condition, _, _ in out)
     pl.semaphore_wait(barrier, expected)
@@ -276,13 +297,12 @@
 def multiply(slab, out_ref):
     half, rows_dev, steps = SIDE * SIDE, slab.shape[1], slab.shape[2]
     left = slab[:half].reshape(half * rows_dev, steps)
-    group = max(1, 256 // rows_dev)
-    for g in range(half // group):
-        right = slab[half + g * group : half + (g + 1) * group]
-        out_ref[:, g * group * rows_dev : (g + 1) * group * rows_dev] = lax.dot_general(
-            left, right.reshape(group * rows_dev, steps), (((1,), (1,)), ((), ())),
-            preferred_element_type=jnp.float32,
-        )
+    group = out_ref.shape[1] // rows_dev
+    right = slab[pl.ds(half + pl.program_id(0) * group, group)]
+    out_ref[...] = lax.dot_general(
+        left, right.reshape(group * rows_dev, steps), (((1,), (1,)), ((), ())),
+        preferred_element_type=jnp.float32,
+    )
 
 
 def on_device(series, lengths, starts):
@@ -290,27 +310,35 @@
     blocks = SIDE * SIDE
     vmem = pl.BlockSpec(memory_space=pltpu.VMEM)
     columns = columns_of(steps)
-    slots = 2 * blocks + 2
+    slots = 2 * blocks + 1
+    in_hbm = [
+        pltpu.with_memory_space_constraint(array, pltpu.HBM)
+        for array in (series, lengths.reshape(1, rows_dev), starts.reshape(1, rows_dev))
+    ]
     slab = pl.pallas_call(
         functools.partial(kernel, columns),
         out_shape=jax.ShapeDtypeStruct((slots, rows_dev, steps), jnp.bfloat16),
-        in_specs=[vmem] * 2,
+        in_specs=[pl.BlockSpec(memory_space=pltpu.HBM)] * 3,
         out_specs=vmem,
         scratch_shapes=[
+            pltpu.VMEM((rows_dev, steps), jnp.float32),
+            pltpu.VMEM((1, rows_dev), jnp.int32),
+            pltpu.VMEM((1, rows_dev), jnp.int32),
             pltpu.SemaphoreType.DMA((slots, len(columns))),
             pltpu.SemaphoreType.DMA((count_sends(),)),
+            pltpu.SemaphoreType.DMA((3,)),
         ],
         compiler_params=pltpu.CompilerParams(
             collective_id=0, has_side_effects=True, vmem_limit_bytes=LIMIT * 2**20
         ),
-    )(series, jnp.stack([lengths, starts]))
+    )(*in_hbm)
     rows = blocks * rows_dev
     return pl.pallas_call(
         multiply,
-        grid=(1,),
+        grid=(OUT_PARTS,),
         out_shape=jax.ShapeDtypeStruct((rows, rows), jnp.float32),
         in_specs=[vmem],
-        out_specs=pl.BlockSpec((rows, rows), lambda i: (i, 0)),
+        out_specs=pl.BlockSpec((rows, rows // OUT_PARTS), lambda i: (0, i)),
         compiler_params=pltpu.CompilerParams(vmem_limit_bytes=LIMIT * 2**20),
     )(slab)
 

time: 76 us -> 65 us (0.86)
  Pallas kernels: 73.8 us -> 64.9 us
  local copies, waits for them, and re-layouts: 1.04 us -> 0 us
    pallas_call x1, Pallas kernels: 67.2 us -> 58.8 us  [on_device(): pl.pallas_call(functools.partial(kernel, columns), out_shape=jax.ShapeDty...]
    unnamed x2 -> x0, local copies, waits for them, and re-layouts: 1.04 us -> none
where the time goes in v2:
time: 65 us; the launch traced here: 64.9 us
  Pallas kernels  64.9 us (100%)
    pallas_call x1, Pallas kernels, on_device(): pl.pallas_call(functools.partial(kernel, columns), out_shape=jax.ShapeDty...  58.8 us
    pallas_call x1, Pallas kernels, on_device(): pl.pallas_call(multiply, grid=(OUT_PARTS,), out_shape=jax.ShapeDtypeStruc...  6.17 us

profile of v2, /device:TPU:1, one launch (start us, length us, event | category | flops | bytes accessed | tf_op | source)
XLA Modules:
  0.0 64.9 jit_solution(10397071801497857416)
XLA Ops:
  0.0 58.8 %shard_map.37.slab = bf16[33,64,2048]{2,1,0:T(8,128)(2,1)S(1)} custom-call(f32[64,2048]{1,0:T(8,128)} %series_hbm.1, s32[1,64]{1,0:T(1,128)} %bitcast.2, s32[1,64]{1,0:T(1,128)} %bitcast.3), custom_call_target="tpu_custom_call" | custom-call | tf_op jit(solution)/shard_map/pallas_call | solution.py:318
  58.8 6.2 %shard_map.38 = f32[1024,1024]{1,0:T(8,128)} custom-call(bf16[33,64,2048]{2,1,0:T(8,128)(2,1)S(1)} %shard_map.37.slab), custom_call_target="tpu_custom_call" | custom-call | tf_op jit(solution)/shard_map/pallas_call | solution.py:336

commit v3 on v2

--- a/solution.py
+++ b/solution.py
@@ -14,19 +14,19 @@
 OUT_PARTS = 4
 MESH = pl.DeviceIdType.MESH
 ORDER = (
-    0, 5, 3, 160, 161, 1, 60, 58, 59, 16, 118, 116, 15, 17, 117, 186, 120, 2, 34, 61, 71,
-    72, 19, 201, 119, 86, 113, 172, 20, 208, 18, 14, 12, 68, 114, 99, 200, 115, 144, 36, 4,
-    122, 224, 111, 13, 112, 45, 170, 100, 225, 121, 9, 142, 35, 97, 203, 57, 98, 11, 23,
-    22, 10, 210, 21, 110, 123, 187, 7, 32, 204, 31, 127, 8, 51, 73, 126, 108, 220, 159,
-    226, 109, 84, 56, 26, 153, 6, 216, 80, 184, 174, 83, 140, 199, 25, 62, 63, 147, 202,
-    228, 236, 217, 189, 95, 148, 138, 124, 33, 171, 205, 211, 178, 222, 212, 135, 82, 182,
-    176, 102, 177, 96, 130, 206, 103, 81, 79, 229, 74, 29, 42, 69, 40, 188, 46, 152, 146,
-    167, 94, 232, 28, 213, 197, 41, 139, 30, 175, 38, 137, 101, 87, 143, 162, 214, 237,
-    163, 132, 105, 76, 47, 44, 169, 75, 221, 166, 54, 194, 37, 158, 128, 125, 43, 218, 155,
-    196, 90, 136, 88, 89, 65, 107, 85, 151, 180, 24, 168, 104, 179, 230, 67, 238, 209, 133,
-    92, 191, 234, 185, 70, 91, 183, 198, 227, 223, 157, 215, 66, 231, 55, 207, 77, 106,
-    192, 181, 219, 49, 27, 173, 235, 78, 165, 134, 131, 145, 50, 39, 195, 190, 156, 141,
-    193, 149, 53, 233, 150, 129, 164, 239, 64, 52, 154, 48, 93,
+    161, 0, 5, 3, 17, 117, 16, 58, 15, 59, 116, 19, 2, 159, 160, 60, 118, 172, 72, 1, 12,
+    13, 142, 20, 34, 71, 187, 18, 185, 121, 4, 186, 208, 115, 22, 114, 120, 11, 23, 73, 10,
+    14, 224, 86, 8, 7, 44, 9, 113, 36, 119, 210, 122, 123, 57, 173, 220, 189, 85, 32, 110,
+    170, 112, 169, 124, 126, 111, 225, 61, 56, 84, 69, 127, 21, 211, 144, 201, 216, 191,
+    168, 100, 226, 25, 174, 108, 158, 28, 51, 125, 203, 74, 184, 66, 190, 182, 152, 83,
+    138, 148, 102, 98, 221, 183, 193, 227, 42, 199, 81, 146, 212, 26, 131, 67, 171, 38,
+    143, 175, 179, 62, 140, 218, 82, 40, 136, 30, 37, 180, 147, 24, 205, 181, 177, 167,
+    157, 228, 232, 155, 29, 178, 137, 236, 209, 88, 176, 197, 222, 96, 33, 166, 106, 109,
+    104, 207, 99, 198, 196, 188, 134, 162, 202, 75, 68, 35, 39, 214, 238, 230, 95, 48, 101,
+    90, 49, 105, 206, 163, 94, 55, 204, 234, 237, 63, 79, 43, 156, 45, 107, 91, 132, 65,
+    153, 97, 80, 233, 135, 192, 64, 195, 223, 76, 231, 77, 6, 78, 129, 27, 215, 200, 31,
+    239, 194, 93, 54, 165, 150, 154, 145, 46, 141, 70, 149, 128, 213, 130, 164, 229, 89,
+    219, 53, 92, 133, 151, 52, 103, 47, 87, 217, 50, 139, 41, 235,
 )
 
 
@@ -202,7 +202,7 @@
 
 
 def kernel(
-    columns, series_hbm, lengths_hbm, starts_hbm, slab,
+    columns, steps, series_hbm, lengths_hbm, starts_hbm, slab,
     series_ref, lengths_ref, starts_ref, recv, send, load,
 ):
     r = lax.axis_index("row")
@@ -235,7 +235,10 @@
     expected = sum(jnp.where(condition, 1, 0) for condition, _, _ in out)
     pl.semaphore_wait(barrier, expected)
 
-    started = []
+    def arrival_of(slot, piece):
+        if piece < 4:
+            return slot * 4 + piece
+        return n * n * 4 + (slot - n * n) * 2 + piece - 4
 
     def part(slot, piece):
         lo, hi = columns[piece]
@@ -246,7 +249,7 @@
             src_ref=part(source, piece),
             dst_ref=part(target, piece),
             send_sem=send.at[index],
-            recv_sem=recv.at[target, piece],
+            recv_sem=recv.at[arrival_of(target, piece)],
             device_id={"row": row, "col": col},
             device_id_type=MESH,
         )
@@ -257,11 +260,11 @@
         else:
             pl.when(condition)(do)
 
-    def handle(wait, sends):
+    def handle(group, wait, sends):
         if wait is not None:
 
             def receive():
-                copy_of(0, wait[0], wait[0], wait[1], r, c).wait_recv()
+                copy_of(group, wait[0], wait[0], wait[1], r, c).wait_recv()
 
             receive()
         for condition, source, target, piece, row, col in sends:
@@ -272,26 +275,50 @@
 
                 guarded(condition, keep)
                 continue
-            index = len(started)
-            copy = functools.partial(copy_of, index, source, target, piece, row, col)
+            copy = functools.partial(copy_of, group, source, target, piece, row, col)
             guarded(condition, lambda copy=copy: copy().start())
-            started.append((condition, copy))
-
+
+    groups = {"near": 0, "side": 0, "far": 0, "left": 1, "over": 1}
     for name, condition, wait, sends, _ in events_of(r, c):
-        before = len(started)
-        guarded(condition, lambda: handle(wait, sends))
-        if condition is not True:
-            started[before:] = [
-                (condition if own is True else condition & own, copy)
-                for own, copy in started[before:]
-            ]
-
-    for condition, copy in started:
-        guarded(condition, lambda copy=copy: copy().wait_send())
-
-
-def count_sends():
-    return sum(len(event[3]) for event in events_of(0, 0))
+        group = groups.get(name[0], 2)
+        guarded(condition, functools.partial(handle, group, wait, sends))
+
+    def sent(group, blocks, tiles):
+        here = slab.at[pl.ds(0, blocks), :, pl.ds(0, tiles * LANES)]
+        pltpu.make_async_remote_copy(
+            src_ref=here, dst_ref=here, send_sem=send.at[group], recv_sem=recv.at[0],
+            device_id={"row": r, "col": c}, device_id_type=MESH,
+        ).wait_send()
+
+    x_tiles, z_tiles = sent_left()
+    sent(0, *x_tiles)
+    z = c % n
+    middle = (z > 0) & (z < n - 1)
+    guarded(middle, lambda: sent(1, *z_tiles[1]))
+    guarded(jnp.logical_not(middle), lambda: sent(1, *z_tiles[0]))
+    rights = 15 + jnp.where(z == 0, 0, 1) + jnp.where(stays_here(r, c), 0, 1)
+    for blocks in (15, 16, 17):
+        guarded(rights == blocks, lambda blocks=blocks: sent(2, blocks, steps // LANES))
+
+
+def stays_here(r, c):
+    n = SIDE
+    y, k = r // 2 % n, r % 2
+    return (r // (2 * n) * 2 * n + (y + n - c % n) % n * 2 + k == c) & (k == 0)
+
+
+def sent_left():
+    near = 2 * ALONG_Z
+    along_x = SIDE * (2 * near + near) + 3 * (16 - near)
+    ends = 16 + 3 * (16 - near)
+    return rectangle(along_x), (rectangle(ends), rectangle(5 * ends))
+
+
+def rectangle(tiles):
+    return next(
+        (tiles // width, width) for width in range(16, 0, -1)
+        if tiles % width == 0 and tiles // width <= 2 * SIDE * SIDE
+    )
 
 
 def multiply(slab, out_ref):
@@ -316,7 +343,7 @@
         for array in (series, lengths.reshape(1, rows_dev), starts.reshape(1, rows_dev))
     ]
     slab = pl.pallas_call(
-        functools.partial(kernel, columns),
+        functools.partial(kernel, columns, steps),
         out_shape=jax.ShapeDtypeStruct((slots, rows_dev, steps), jnp.bfloat16),
         in_specs=[pl.BlockSpec(memory_space=pltpu.HBM)] * 3,
         out_specs=vmem,
@@ -324,8 +351,8 @@
             pltpu.VMEM((rows_dev, steps), jnp.float32),
             pltpu.VMEM((1, rows_dev), jnp.int32),
             pltpu.VMEM((1, rows_dev), jnp.int32),
-            pltpu.SemaphoreType.DMA((slots, len(columns))),
-            pltpu.SemaphoreType.DMA((count_sends(),)),
+            pltpu.SemaphoreType.DMA((blocks * 4 + (blocks + 1) * 2,)),
+            pltpu.SemaphoreType.DMA((3,)),
             pltpu.SemaphoreType.DMA((3,)),
         ],
         compiler_params=pltpu.CompilerParams(

time: 65 us -> 59.4 us (0.914); the launches traced: 64.9 us -> 58.5 us
  Pallas kernels: 64.9 us -> 58.5 us
    pallas_call x1, Pallas kernels: 58.8 us -> 52.3 us  [on_device(): pl.pallas_call(functools.partial(kernel, columns, steps), out_shape=jax.S...]
where the time goes in v3:
time: 59.4 us; the launch traced here: 58.5 us
  Pallas kernels  58.5 us (98%)
    pallas_call x1, Pallas kernels, on_device(): pl.pallas_call(functools.partial(kernel, columns, steps), out_shape=jax.S...  52.3 us
    pallas_call x1, Pallas kernels, on_device(): pl.pallas_call(multiply, grid=(OUT_PARTS,), out_shape=jax.ShapeDtypeStruc...  6.17 us

profile of v3, /device:TPU:1, one launch (start us, length us, event | category | flops | bytes accessed | tf_op | source)
XLA Modules:
  0.0 58.5 jit_solution(18128533027883467635)
XLA Ops:
  0.0 52.3 %shard_map.37.slab = bf16[33,64,2048]{2,1,0:T(8,128)(2,1)S(1)} custom-call(f32[64,2048]{1,0:T(8,128)} %series_hbm.1, s32[1,64]{1,0:T(1,128)} %bitcast.2, s32[1,64]{1,0:T(1,128)} %bitcast.3), custom_call_target="tpu_custom_call" | custom-call | tf_op jit(solution)/shard_map/pallas_call | solution.py:345
  52.3 6.2 %shard_map.38 = f32[1024,1024]{1,0:T(8,128)} custom-call(bf16[33,64,2048]{2,1,0:T(8,128)(2,1)S(1)} %shard_map.37.slab), custom_call_target="tpu_custom_call" | custom-call | tf_op jit(solution)/shard_map/pallas_call | solution.py:363

commit v4 on v3

--- a/solution.py
+++ b/solution.py
@@ -11,7 +11,7 @@
 SIDE = 4
 ALONG_Z = 7
 LIMIT = 32
-OUT_PARTS = 4
+AHEAD = (0, 3, 1)
 MESH = pl.DeviceIdType.MESH
 ORDER = (
     161, 0, 5, 3, 17, 117, 16, 58, 15, 59, 116, 19, 2, 159, 160, 60, 118, 172, 72, 1, 12,
@@ -163,6 +163,7 @@
                 events.append((("across", j, dy, half), True, (slot, half), [], []))
     if ORDER:
         events = [events[i] for i in ORDER]
+    events = [e for e in events if e[3]] + [e for e in events if not e[3]]
     waited = set()
     for i, (name, valid, wait, sends, needs) in enumerate(events):
         if name[0] in ("left", "near", "side", "far", "over"):
@@ -202,7 +203,7 @@
 
 
 def kernel(
-    columns, steps, series_hbm, lengths_hbm, starts_hbm, slab,
+    columns, steps, series_hbm, lengths_hbm, starts_hbm, slab, partial,
     series_ref, lengths_ref, starts_ref, recv, send, load,
 ):
     r = lax.axis_index("row")
@@ -279,9 +280,30 @@
             guarded(condition, lambda copy=copy: copy().start())
 
     groups = {"near": 0, "side": 0, "far": 0, "left": 1, "over": 1}
-    for name, condition, wait, sends, _ in events_of(r, c):
-        group = groups.get(name[0], 2)
-        guarded(condition, functools.partial(handle, group, wait, sends))
+    events = events_of(r, c)
+    for name, condition, wait, sends, _ in events:
+        if sends:
+            group = groups.get(name[0], 2)
+            guarded(condition, functools.partial(handle, group, wait, sends))
+
+    def arrive(kind, second, dx=None):
+        for name, condition, wait, sends, _ in events:
+            if sends or name[0] != kind or wait is None:
+                continue
+            if kind == "across" and name[3] - 4 != second:
+                continue
+            if kind == "left" and (name[1] != dx or name[3] // 2 != second):
+                continue
+            guarded(condition, functools.partial(handle, 2, wait, ()))
+
+    arrive("across", 0)
+    for dx in AHEAD:
+        arrive("left", 0, dx)
+        multiply_part(slab, (c // n + dx) % n, 0, steps // 2, None, partial)
+    arrive("left", 0, 2)
+    for dx in AHEAD + (2,):
+        arrive("left", 1, dx)
+    arrive("across", 1)
 
     def sent(group, blocks, tiles):
         here = slab.at[pl.ds(0, blocks), :, pl.ds(0, tiles * LANES)]
@@ -321,15 +343,46 @@
     )
 
 
-def multiply(slab, out_ref):
-    half, rows_dev, steps = SIDE * SIDE, slab.shape[1], slab.shape[2]
-    left = slab[:half].reshape(half * rows_dev, steps)
-    group = out_ref.shape[1] // rows_dev
-    right = slab[pl.ds(half + pl.program_id(0) * group, group)]
-    out_ref[...] = lax.dot_general(
-        left, right.reshape(group * rows_dev, steps), (((1,), (1,)), ((), ())),
-        preferred_element_type=jnp.float32,
-    )
+def multiply_part(slab, x, lo, hi, before, target, written=None):
+    rows = SIDE * slab.shape[1]
+    here = pl.ds(lo, hi - lo)
+    left = slab[pl.ds(x * SIDE, SIDE), :, here]
+    left = left.reshape(rows, left.shape[2])
+    there = pl.ds(pl.multiple_of(x * rows, rows), rows)
+    for g in range(SIDE):
+        right = slab[SIDE * SIDE + g * SIDE : SIDE * SIDE + (g + 1) * SIDE, :, here]
+        product = lax.dot_general(
+            left, right.reshape(rows, right.shape[2]), (((1,), (1,)), ((), ())),
+            preferred_element_type=jnp.float32,
+        )
+        columns = slice(g * rows, (g + 1) * rows)
+        if before is not None:
+            product = product + before[there, columns]
+        target[there, columns] = product
+        if written is not None:
+            written(there, columns, g)
+
+
+def multiply(slab, partial, out_hbm, out_ref, done):
+    n = SIDE
+    x = lax.axis_index("col") // n
+    copies = []
+    for i, dx in enumerate(AHEAD + (2,)):
+
+        def written(there, columns, g, i=i):
+            copy = pltpu.make_async_copy(
+                out_ref.at[there, columns], out_hbm.at[there, columns], done.at[i * n + g]
+            )
+            copy.start()
+            copies.append(copy)
+
+        ahead = dx in AHEAD
+        multiply_part(
+            slab, (x + dx) % n, slab.shape[2] // 2 if ahead else 0, slab.shape[2],
+            partial if ahead else None, out_ref, written,
+        )
+    for copy in copies:
+        copy.wait()
 
 
 def on_device(series, lengths, starts):
@@ -342,11 +395,15 @@
         pltpu.with_memory_space_constraint(array, pltpu.HBM)
         for array in (series, lengths.reshape(1, rows_dev), starts.reshape(1, rows_dev))
     ]
-    slab = pl.pallas_call(
+    rows = blocks * rows_dev
+    slab, partial = pl.pallas_call(
         functools.partial(kernel, columns, steps),
-        out_shape=jax.ShapeDtypeStruct((slots, rows_dev, steps), jnp.bfloat16),
+        out_shape=(
+            jax.ShapeDtypeStruct((slots, rows_dev, steps), jnp.bfloat16),
+            jax.ShapeDtypeStruct((rows, rows), jnp.float32),
+        ),
         in_specs=[pl.BlockSpec(memory_space=pltpu.HBM)] * 3,
-        out_specs=vmem,
+        out_specs=(vmem, vmem),
         scratch_shapes=[
             pltpu.VMEM((rows_dev, steps), jnp.float32),
             pltpu.VMEM((1, rows_dev), jnp.int32),
@@ -359,15 +416,17 @@
             collective_id=0, has_side_effects=True, vmem_limit_bytes=LIMIT * 2**20
         ),
     )(*in_hbm)
-    rows = blocks * rows_dev
     return pl.pallas_call(
         multiply,
-        grid=(OUT_PARTS,),
         out_shape=jax.ShapeDtypeStruct((rows, rows), jnp.float32),
-        in_specs=[vmem],
-        out_specs=pl.BlockSpec((rows, rows // OUT_PARTS), lambda i: (0, i)),
+        in_specs=[vmem] * 2,
+        out_specs=pl.BlockSpec(memory_space=pltpu.HBM),
+        scratch_shapes=[
+            pltpu.VMEM((rows, rows), jnp.float32),
+            pltpu.SemaphoreType.DMA((blocks,)),
+        ],
         compiler_params=pltpu.CompilerParams(vmem_limit_bytes=LIMIT * 2**20),
-    )(slab)
+    )(slab, partial)
 
 
 def solution(mesh):

time: 59.4 us -> 57.9 us (0.975)
  Pallas kernels: 58.5 us -> 57.5 us
    pallas_call x2, Pallas kernels: 58.5 us -> 57.5 us  [the longest x1 53.4 us: on_device(): pl.pallas_call(functools.partial(kernel, columns, steps), out_shape=(jax....]
where the time goes in v4:
time: 57.9 us; the launch traced here: 57.5 us
  Pallas kernels  57.5 us (99%)
    pallas_call x1, Pallas kernels, on_device(): pl.pallas_call(functools.partial(kernel, columns, steps), out_shape=(jax....  53.4 us
    pallas_call x1, Pallas kernels, on_device(): pl.pallas_call(multiply, out_shape=jax.ShapeDtypeStruct((rows, rows), jnp...  4.09 us

profile of v4, /device:TPU:1, one launch (start us, length us, event | category | flops | bytes accessed | tf_op | source)
XLA Modules:
  0.0 57.5 jit_solution(9809566996852994937)
XLA Ops:
  0.0 53.4 %shard_map.37 = (bf16[33,64,2048]{2,1,0:T(8,128)(2,1)S(1)}, f32[1024,1024]{1,0:T(8,128)S(1)}) custom-call(f32[64,2048]{1,0:T(8,128)} %series_hbm.1, s32[1,64]{1,0:T(1,128)} %bitcast.2, s32[1,64]{1,0:T(1,128)} %bitcast.3), custom_call_target="tpu_custom_call" | custom-call | tf_op jit(solution)/shard_map/pallas_call | solution.py:399
  53.4 4.1 %shard_map.38 = f32[1024,1024]{1,0:T(8,128)} custom-call(bf16[33,64,2048]{2,1,0:T(8,128)(2,1)S(1)} %get-tuple-element.7.slab, f32[1024,1024]{1,0:T(8,128)S(1)} %get-tuple-element.8.partial), custom_call_target="tpu_custom_call" | custom-call | tf_op jit(solution)/shard_map/pallas_call | solution.py:419

commit v5 on v4

--- a/solution.py
+++ b/solution.py
@@ -14,19 +14,19 @@
 AHEAD = (0, 3, 1)
 MESH = pl.DeviceIdType.MESH
 ORDER = (
-    161, 0, 5, 3, 17, 117, 16, 58, 15, 59, 116, 19, 2, 159, 160, 60, 118, 172, 72, 1, 12,
-    13, 142, 20, 34, 71, 187, 18, 185, 121, 4, 186, 208, 115, 22, 114, 120, 11, 23, 73, 10,
-    14, 224, 86, 8, 7, 44, 9, 113, 36, 119, 210, 122, 123, 57, 173, 220, 189, 85, 32, 110,
-    170, 112, 169, 124, 126, 111, 225, 61, 56, 84, 69, 127, 21, 211, 144, 201, 216, 191,
-    168, 100, 226, 25, 174, 108, 158, 28, 51, 125, 203, 74, 184, 66, 190, 182, 152, 83,
-    138, 148, 102, 98, 221, 183, 193, 227, 42, 199, 81, 146, 212, 26, 131, 67, 171, 38,
-    143, 175, 179, 62, 140, 218, 82, 40, 136, 30, 37, 180, 147, 24, 205, 181, 177, 167,
-    157, 228, 232, 155, 29, 178, 137, 236, 209, 88, 176, 197, 222, 96, 33, 166, 106, 109,
-    104, 207, 99, 198, 196, 188, 134, 162, 202, 75, 68, 35, 39, 214, 238, 230, 95, 48, 101,
-    90, 49, 105, 206, 163, 94, 55, 204, 234, 237, 63, 79, 43, 156, 45, 107, 91, 132, 65,
-    153, 97, 80, 233, 135, 192, 64, 195, 223, 76, 231, 77, 6, 78, 129, 27, 215, 200, 31,
-    239, 194, 93, 54, 165, 150, 154, 145, 46, 141, 70, 149, 128, 213, 130, 164, 229, 89,
-    219, 53, 92, 133, 151, 52, 103, 47, 87, 217, 50, 139, 41, 235,
+    3, 117, 0, 59, 118, 58, 5, 15, 116, 16, 17, 161, 2, 160, 60, 20, 1, 19, 34, 171, 71,
+    18, 120, 187, 12, 186, 4, 119, 142, 208, 14, 13, 224, 36, 22, 144, 21, 45, 209, 114, 9,
+    11, 159, 113, 115, 212, 172, 201, 10, 8, 7, 210, 32, 226, 123, 121, 232, 100, 23, 111,
+    189, 124, 26, 216, 174, 228, 25, 110, 99, 122, 72, 57, 86, 218, 126, 38, 203, 39, 30,
+    98, 102, 140, 175, 108, 162, 74, 109, 83, 40, 185, 101, 28, 44, 61, 225, 184, 41, 234,
+    69, 173, 146, 176, 56, 76, 68, 220, 51, 153, 96, 50, 213, 163, 104, 27, 94, 88, 148,
+    181, 214, 205, 127, 230, 62, 112, 217, 130, 152, 138, 136, 128, 6, 199, 131, 170, 202,
+    63, 222, 164, 90, 135, 143, 75, 35, 178, 158, 196, 188, 84, 73, 236, 89, 93, 182, 238,
+    179, 29, 85, 65, 192, 48, 194, 183, 78, 229, 151, 42, 91, 165, 227, 167, 97, 177, 133,
+    204, 231, 54, 92, 70, 37, 168, 207, 52, 190, 215, 125, 46, 206, 219, 156, 33, 64, 137,
+    95, 132, 67, 166, 47, 211, 43, 235, 103, 195, 239, 157, 197, 105, 55, 147, 193, 66, 87,
+    139, 77, 31, 145, 233, 134, 82, 191, 154, 198, 155, 53, 180, 200, 150, 223, 237, 24,
+    221, 129, 107, 49, 169, 79, 141, 81, 149, 80, 106,
 )
 
 
@@ -103,8 +103,7 @@
                  col_at(home_x, home_z)),
                 (here, source, slot, half, None, None),
             ]
-            for row in (row_at(zh, y + 2, k), row_at(zh, y + 1, k), row_at(zh, y + n - 1, k),
-                        row_at(zh, y, 1 - k)):
+            for row in (row_at(zh, y + 1, k), row_at(zh, y + n - 1, k), row_at(zh, y, 1 - k)):
                 sends.append((here, slot, slot, half, row, c))
             valid, wait = (z != 0, (2 * n * n, half)) if kind == "moved" else (z == 0, None)
             events.append(((kind, half), valid, wait, sends, []))
@@ -151,8 +150,11 @@
                 across = (True, slot, slot, half, row_at(zh, y, 1 - k), c)
                 sends = []
                 if dy == 0:
-                    beyond = (True, slot, slot, half, row_at(zh, y + 2, k), c)
-                    sends = [beyond, up, down]
+                    sends = [up, down] if half == 4 else [down, up]
+                elif dy == 3 and half == 4:
+                    sends = [up]
+                elif dy == 1 and half == 5:
+                    sends = [down]
                 valid = True
                 if dy == 0 and j == 0:
                     valid = pick((k == 0) & (panel == c), 0, 1) == 1
@@ -181,7 +183,7 @@
     x, z = c // n, c % n
     around = [(True, r, (c + n) % (n * n)), (True, r, (c + 3 * n) % (n * n))]
     around += [(z < n - 1, r, c + 1), (z > 0, r, c - 1)]
-    for dy in (1, 2, n - 1):
+    for dy in (1, n - 1):
         around.append((True, zh * 2 * n + (y + dy) % n * 2 + k, c))
     around.append((True, r + 1 - 2 * k, c))
     into, out = list(around), list(around)

time: 57.9 us -> 55.9 us (0.965)
  Pallas kernels: 57.5 us -> 55.8 us
    pallas_call x1, Pallas kernels: 53.4 us -> 51.7 us  [on_device(): pl.pallas_call(functools.partial(kernel, columns, steps), out_shape=(jax....]
where the time goes in v5:
time: 55.9 us; the launch traced here: 55.8 us
  Pallas kernels  55.8 us (100%)
    pallas_call x1, Pallas kernels, on_device(): pl.pallas_call(functools.partial(kernel, columns, steps), out_shape=(jax....  51.7 us
    pallas_call x1, Pallas kernels, on_device(): pl.pallas_call(multiply, out_shape=jax.ShapeDtypeStruct((rows, rows), jnp...  4.09 us

profile of v5, /device:TPU:1, one launch (start us, length us, event | category | flops | bytes accessed | tf_op | source)
XLA Modules:
  0.0 55.8 jit_solution(17432290373583956303)
XLA Ops:
  0.0 51.7 %shard_map.37 = (bf16[33,64,2048]{2,1,0:T(8,128)(2,1)S(1)}, f32[1024,1024]{1,0:T(8,128)S(1)}) custom-call(f32[64,2048]{1,0:T(8,128)} %series_hbm.1, s32[1,64]{1,0:T(1,128)} %bitcast.2, s32[1,64]{1,0:T(1,128)} %bitcast.3), custom_call_target="tpu_custom_call" | custom-call | tf_op jit(solution)/shard_map/pallas_call | solution.py:401
  51.7 4.1 %shard_map.38 = f32[1024,1024]{1,0:T(8,128)} custom-call(bf16[33,64,2048]{2,1,0:T(8,128)(2,1)S(1)} %get-tuple-element.7.slab, f32[1024,1024]{1,0:T(8,128)S(1)} %get-tuple-element.8.partial), custom_call_target="tpu_custom_call" | custom-call | tf_op jit(solution)/shard_map/pallas_call | solution.py:421

commit v6 on v5

--- a/solution.py
+++ b/solution.py
@@ -11,7 +11,7 @@
 SIDE = 4
 ALONG_Z = 7
 LIMIT = 32
-AHEAD = (0, 3, 1)
+AHEAD = (0, 1, 3)
 MESH = pl.DeviceIdType.MESH
 ORDER = (
     3, 117, 0, 59, 118, 58, 5, 15, 116, 16, 17, 161, 2, 160, 60, 20, 1, 19, 34, 171, 71,

time: 55.9 us -> 55.9 us (level)
  no operation moved by 1% of the time
where the time goes in v6:
time: 55.9 us; the launch traced here: 55.8 us
  Pallas kernels  55.8 us (100%)
    pallas_call x1, Pallas kernels, on_device(): pl.pallas_call(functools.partial(kernel, columns, steps), out_shape=(jax....  51.7 us
    pallas_call x1, Pallas kernels, on_device(): pl.pallas_call(multiply, out_shape=jax.ShapeDtypeStruct((rows, rows), jnp...  4.1 us

profile of v6, /device:TPU:1, one launch (start us, length us, event | category | flops | bytes accessed | tf_op | source)
XLA Modules:
  0.0 55.8 jit_solution(17307434875571252622)
XLA Ops:
  0.0 51.7 %shard_map.37 = (bf16[33,64,2048]{2,1,0:T(8,128)(2,1)S(1)}, f32[1024,1024]{1,0:T(8,128)S(1)}) custom-call(f32[64,2048]{1,0:T(8,128)} %series_hbm.1, s32[1,64]{1,0:T(1,128)} %bitcast.2, s32[1,64]{1,0:T(1,128)} %bitcast.3), custom_call_target="tpu_custom_call" | custom-call | tf_op jit(solution)/shard_map/pallas_call | solution.py:401
  51.7 4.1 %shard_map.38 = f32[1024,1024]{1,0:T(8,128)} custom-call(bf16[33,64,2048]{2,1,0:T(8,128)(2,1)S(1)} %get-tuple-element.7.slab, f32[1024,1024]{1,0:T(8,128)S(1)} %get-tuple-element.8.partial), custom_call_target="tpu_custom_call" | custom-call | tf_op jit(solution)/shard_map/pallas_call | solution.py:421
